TPU v7x, 32 devices: a whole 2x2x4 slice. The times are simulated.
32 devices in a mesh: grp: 2 (over core), dev: 16 (over z, y, x).
Axes of the slice: x: 2, y: 2, z: 4, core: 2. Of those that a mesh axis runs over, the one named last changes fastest.
Arguments:
- emb_table: float32 [16384, 512], P(('grp', 'dev')), may hold values from -1.5 to 1.5
- adagrad_state: float32 [16384], P(('grp', 'dev')), may hold values from 0.05 to 1
- send_rows: int32 [32, 32, 32], P(('grp', 'dev')), may hold values from 0 to 511, as said below
- lookup_slot: int32 [8192, 8], P(('grp', 'dev')), may hold values from 0 to 1023, as said below
- seq_lengths: int32 [32, 2], P(('grp', 'dev')), may hold values from 0 to 256, as said below
- in_weight: bfloat16 [512, 2048], replicated, may hold values from -0.25 to 0.25
- out_weight: bfloat16 [512, 512], replicated, may hold values from -0.25 to 0.25
- norm_gain: float32 [512], replicated, may hold values from 0.5 to 1.5
- out_grad: bfloat16 [8192, 512], P(('grp', 'dev')), may hold values from -3 to 3
Outputs:
- layer_out: bfloat16 [8192, 512], P(('grp', 'dev'))
- table_new: float32 [16384, 512], P(('grp', 'dev'))
- state_new: float32 [16384], P(('grp', 'dev'))
- grad_in_weight: float32 [512, 2048], replicated
- grad_out_weight: float32 [512, 512], replicated
- grad_norm_gain: float32 [512], replicated
Inputs may be any that keep to these rules, and one draw needn't show every extreme that they name: For each table shard o and device d, the 32 entries of send_rows[o, d] are distinct rows of the shard; every row of a shard is listed for exactly two different devices. `lookup_slot`: each device reads every one of its 1024 received rows at least once. `seq_lengths`: the 2 lengths of each device sum to 256; the first is at least 64, and a length of 0 means an empty slot, so a device holds one or two sequences.
All inputs are finite; a program needn't handle non-finite values.
Results may differ from a plain program's by a relative error of at most 0.012.
Values may be sent and summed in bfloat16 or wider, within the bound.
A program may use at most 64 MiB of HBM per device.

v0:
```python
from functools import partial
import math

import jax
import jax.numpy as jnp
from jax import lax
from jax.sharding import PartitionSpec as P

HEADS = 4


learn_rate = 0.2
norm_eps = 1e-05
adagrad_eps = 1e-08


def narrow(pattern, left_op, right_op):
    return jnp.einsum(pattern, left_op, right_op, preferred_element_type=jnp.float32)


def build_mask(lengths, slot_total):
    positions = jnp.arange(slot_total, dtype=jnp.int32)
    bounds = jnp.cumsum(lengths, dtype=jnp.int32)
    sequence_id = jnp.sum(
        (positions[:, None] >= bounds[None, :]).astype(jnp.int32), axis=1, dtype=jnp.int32
    )
    same_seq = sequence_id[:, None] == sequence_id[None, :]
    causal = positions[None, :] <= positions[:, None]
    return (same_seq & causal).astype(jnp.float32)


def attend(preact, norm_gain, seq_mask, head_count, product):
    activated = jax.nn.silu(preact).astype(jnp.bfloat16)
    tokens_here, stacked = activated.shape
    model_width = stacked // 4
    head_dim = model_width // head_count
    gate_part = activated[:, :model_width]
    values = activated[:, model_width : 2 * model_width].reshape(tokens_here, head_count, head_dim)
    queries = activated[:, 2 * model_width : 3 * model_width].reshape(
        tokens_here, head_count, head_dim
    )
    keys_all = activated[:, 3 * model_width :].reshape(tokens_here, head_count, head_dim)
    scores = product("thd,shd->hts", queries, keys_all) * (1.0 / math.sqrt(head_dim))
    weights = (jax.nn.silu(scores) * seq_mask).astype(jnp.bfloat16)
    attended = product("hts,shd->thd", weights, values).reshape(tokens_here, model_width)
    center = attended - jnp.mean(attended, axis=1, keepdims=True)
    spread = jnp.mean(center * center, axis=1, keepdims=True)
    normed = center * lax.rsqrt(spread + norm_eps)
    return (normed * norm_gain * gate_part.astype(jnp.float32)).astype(jnp.bfloat16)


def pool_rows(received, token_slots):
    pooled_sum = jnp.zeros((token_slots.shape[0], received.shape[1]), jnp.float32)
    for feature in range(token_slots.shape[1]):
        pooled_sum = pooled_sum + received[token_slots[:, feature]].astype(jnp.float32)
    return pooled_sum.astype(jnp.bfloat16)


def presum(d_pooled, token_slots, slot_total):
    spread = jnp.broadcast_to(
        d_pooled[:, None, :], (token_slots.shape[0], token_slots.shape[1], d_pooled.shape[1])
    )
    return jax.ops.segment_sum(
        spread.reshape(-1, d_pooled.shape[1]), token_slots.reshape(-1), num_segments=slot_total
    )


def dense_step(pooled, in_weight, out_weight, norm_gain, out_grad, seq_mask, head_count, product):
    preact = jnp.dot(pooled, in_weight, preferred_element_type=jnp.float32)
    mixed_out, pullback = jax.vjp(
        partial(attend, seq_mask=seq_mask, head_count=head_count, product=product),
        preact,
        norm_gain,
    )
    layer_out = (
        jnp.dot(mixed_out, out_weight, preferred_element_type=jnp.float32)
        + pooled.astype(jnp.float32)
    ).astype(jnp.bfloat16)
    grad_wout = jnp.dot(mixed_out.T, out_grad, preferred_element_type=jnp.float32)
    d_mixed = jnp.dot(out_grad, out_weight.T, preferred_element_type=jnp.float32).astype(
        jnp.bfloat16
    )
    d_preact, d_gain = pullback(d_mixed)
    d_low = d_preact.astype(jnp.bfloat16)
    grad_win = jnp.dot(pooled.T, d_low, preferred_element_type=jnp.float32)
    d_pooled = jnp.dot(d_low, in_weight.T, preferred_element_type=jnp.float32) + out_grad.astype(
        jnp.float32
    )
    return (layer_out, grad_win, grad_wout, d_gain, d_pooled)


def body(
    emb_table,
    adagrad_state,
    send_rows,
    lookup_slot,
    seq_lengths,
    in_weight,
    out_weight,
    norm_gain,
    out_grad,
):
    row_lists = send_rows[0]
    peer_count, slot_count = row_lists.shape
    row_width = emb_table.shape[1]
    outgoing = emb_table[row_lists].astype(jnp.bfloat16)
    incoming = lax.all_to_all(outgoing, ("grp", "dev"), split_axis=0, concat_axis=0, tiled=True)
    received = incoming.reshape(peer_count * slot_count, row_width)
    pooled = pool_rows(received, lookup_slot)
    seq_mask = build_mask(seq_lengths[0], lookup_slot.shape[0])
    layer_out, grad_win, grad_wout, d_gain, d_pooled = dense_step(
        pooled, in_weight, out_weight, norm_gain, out_grad, seq_mask, HEADS, narrow
    )
    summed = lax.psum((grad_win, grad_wout, d_gain), ("grp", "dev"))
    row_grad = presum(d_pooled, lookup_slot, peer_count * slot_count).reshape(
        peer_count, slot_count, row_width
    )
    arriving = lax.all_to_all(
        row_grad.astype(jnp.bfloat16), ("grp", "dev"), split_axis=0, concat_axis=0, tiled=True
    ).astype(row_grad.dtype)
    grad_rows = jax.ops.segment_sum(
        arriving.reshape(peer_count * slot_count, row_width),
        row_lists.reshape(-1),
        num_segments=emb_table.shape[0],
    )
    state_new = adagrad_state + jnp.mean(grad_rows * grad_rows, axis=1)
    table_new = emb_table - learn_rate * grad_rows / (jnp.sqrt(state_new)[:, None] + adagrad_eps)
    grad_scale = 1.0 / math.sqrt(lookup_slot.shape[0] * peer_count)
    return (
        layer_out,
        table_new,
        state_new,
        summed[0] * grad_scale,
        summed[1] * grad_scale,
        summed[2] * grad_scale,
    )


def solution(mesh):
    in_specs = (
        P(("grp", "dev"), None),
        P(("grp", "dev")),
        P(("grp", "dev"), None, None),
        P(("grp", "dev"), None),
        P(("grp", "dev"), None),
        P(),
        P(),
        P(),
        P(("grp", "dev"), None),
    )
    out_specs = (P(("grp", "dev"), None), P(("grp", "dev"), None), P(("grp", "dev")), P(), P(), P())
    return jax.shard_map(body, mesh=mesh, in_specs=in_specs, out_specs=out_specs, check_vma=False)
```

profile of v0, /device:TPU:0, one launch (start us, length us, event | category | flops | bytes accessed | tf_op | source)
XLA Modules:
  0.0 296.3 jit_solution(680419519024943703)
XLA Ops:
  7.2 0.9 compare_select_fusion
  8.1 6.3 %gather_fusion = bf16[1024,512]{1,0:T(8,128)(2,1)} fusion(f32[512,512]{1,0:T(8,128)} %param.9, s32[1024]{0:T(1024)S(1)} %broadcast_clamp_fusion), kind=kCustom, calls=%fused_computation | custom fusion | bytes 2101248 | tf_op jit(solution)/shard_map/gather | solution.py:106
  14.5 7.3 %all-to-all-start = ((bf16[32,32,512]{2,1,0:T(8,128)(2,1)}), bf16[32,32,512]{2,1,0:T(8,128)(2,1)S(1)}, u32[]{:S(2)}, u32[]{:S(2)}) async-start(bf16[32,32,512]{2,1,0:T(8,128)(2,1)} %bitcast.84), calls=%async_computation | async-start | bytes 2097152 | tf_op jit(solution)/shard_map/all_to_all | solution.py:107
  22.5 0.8 fusion.24
  23.3 26.6 %all-to-all-done = bf16[32,32,512]{2,1,0:T(8,128)(2,1)S(1)} async-done(((bf16[32,32,512]{2,1,0:T(8,128)(2,1)}), bf16[32,32,512]{2,1,0:T(8,128)(2,1)S(1)}, u32[]{:S(2)}, u32[]{:S(2)}) %all-to-all-start) | async-done | bytes 1048608 | tf_op jit(solution)/shard_map/all_to_all | solution.py:107
  49.9 1.9 gather_fusion.8
  51.7 1.9 gather_fusion.7
  53.6 1.9 gather_fusion.6
  55.4 1.8 gather_fusion.5
  57.3 1.8 gather_fusion.4
  59.1 1.8 gather_fusion.3
  60.9 1.9 gather_fusion.2
  62.8 1.9 gather_fusion.1
  64.7 1.8 add_convert_fusion
  66.4 2.1 multiply_convert_fusion
  68.5 1.0 slice_bitcast_fusion
  69.5 1.8 copy.60
  71.3 1.8 copy.59
  73.1 2.7 multiply_convert_fusion.1
  75.7 0.3 fusion.30
  76.2 0.3 copy-done.3
  76.7 1.7 multiply_reduce_fusion.1
  78.4 2.1 fusion.29
  80.8 0.9 fusion.35
  81.8 2.1 fusion.14
  83.9 1.0 fusion.33
  84.9 0.9 fusion.34
  85.8 1.8 copy.58
  87.6 1.8 copy.56
  89.4 0.8 copy.57
  90.3 2.7 fusion.3
  93.0 1.5 convolution_add_fusion
  94.5 2.9 fusion.31
  97.5 14.6 %scatter_custom_fusion = f32[1024,512]{1,0:T(8,128)} fusion(s32[2048]{0:T(1024)S(1)} %reshape.269, f32[256,512]{1,0:T(8,128)} %convolution_add_fusion, f32[]{:T(128)} %constant.18.clone.1), kind=kCustom, calls=%fused_computation.11 | custom fusion | flops 1048576 | bytes 2621444 | tf_op jit(solution)/shard_map/scatter-add | solution.py:63
  112.1 2.8 convert_element_type.139
  114.9 3.4 %all-to-all-start.1 = ((bf16[32,32,512]{2,1,0:T(8,128)(2,1)}), bf16[32,32,512]{2,1,0:T(8,128)(2,1)}, u32[]{:S(2)}, u32[]{:S(2)}) async-start(bf16[32,32,512]{2,1,0:T(8,128)(2,1)} %bitcast.25), calls=%async_computation.1 | async-start | bytes 2097152 | tf_op jit(solution)/shard_map/all_to_all | solution.py:118
  118.3 1.3 fusion.32
  119.7 0.7 copy-done.14
  120.5 51.2 %psum.23 = f32[512]{0:T(512)S(1)} all-reduce(f32[512]{0:T(512)S(1)} %get-tuple-element.6), channel_id=1, replica_groups=mesh['grp'=2,'dev'=16] {'grp','dev'}, use_global_device_ids=true, to_apply=%region_12.13 | all-reduce | flops 512 | bytes 4096 | tf_op jit(solution)/shard_map/psum | solution.py:114
  171.6 0.6 broadcast_multiply_fusion.2
  172.2 2.2 fusion.10
  174.4 8.2 %scatter_custom_fusion.1 = f32[512,512]{1,0:T(8,128)} fusion(s32[1024]{0:T(1024)S(1)} %reshape.277, bf16[1024,512]{1,0:T(8,128)(2,1)} %bitcast.31, f32[]{:T(128)} %constant.18.clone.1), kind=kCustom, calls=%fused_computation.19 | custom fusion | flops 1048576 | bytes 2097156 | tf_op jit(solution)/shard_map/scatter-add | solution.py:121
  182.6 1.4 multiply_reduce_fusion
  184.0 0.6 sqrt_add_fusion
  184.6 2.4 divide_subtract_fusion
  187.0 96.3 %all-reduce.7.cloned.1.call-done = (f32[512,2048]{1,0:T(8,128)}, f32[512,512]{1,0:T(8,128)}) async-done(((f32[512,2048]{1,0:T(8,128)}, f32[512,512]{1,0:T(8,128)}), (f32[512,2048]{1,0:T(8,128)}, f32[512,512]{1,0:T(8,128)})) %all-reduce.7.cloned.1.call-update) | async-done | bytes 5242896 | tf_op jit(solution)/shard_map/psum | solution.py:114
  283.3 5.0 %broadcast_multiply_fusion = f32[512,2048]{1,0:T(8,128)} fusion(f32[512,2048]{1,0:T(8,128)} %get-tuple-element.8), kind=kLoop, calls=%fused_computation.21 | loop fusion | flops 1048576 | bytes 8388608 | tf_op jit(solution)/shard_map/mul | solution.py:133
  288.4 1.1 broadcast_multiply_fusion.1
  (63 shorter events, 1.4 us)
Async XLA Ops:
  7.2 59.3 %copy-start = (bf16[512,2048]{1,0:T(8,128)(2,1)S(1)}, bf16[512,2048]{1,0:T(8,128)(2,1)}, u32[]{:S(2)}) copy-start(bf16[512,2048]{1,0:T(8,128)(2,1)} %param.14) | copy-start | bytes 6291460
  14.5 7.3 %copy-start.15 = (s32[256,8]{0,1:T(8,128)S(1)}, s32[256,8]{0,1:T(8,128)}, u32[]{:S(2)}) copy-start(s32[256,8]{0,1:T(8,128)} %param.12) | copy-start | bytes 24580
  14.5 7.6 %copy-start.18 = (s32[1,2]{1,0:T(1,128)S(1)}, s32[1,2]{1,0:T(1,128)}, u32[]{:S(2)}) copy-start(s32[1,2]{1,0:T(1,128)} %param.13) | copy-start | bytes 28
  14.5 35.4 %all-to-all-start = ((bf16[32,32,512]{2,1,0:T(8,128)(2,1)}), bf16[32,32,512]{2,1,0:T(8,128)(2,1)S(1)}, u32[]{:S(2)}, u32[]{:S(2)}) async-start(bf16[32,32,512]{2,1,0:T(8,128)(2,1)} %bitcast.84), calls=%async_computation | async-start | bytes 2097152 | tf_op jit(solution)/shard_map/all_to_all | solution.py:107
  68.5 4.6 %copy-start.5 = (bf16[256,2048]{1,0:T(8,128)(2,1)}, bf16[256,2048]{1,0:T(8,128)(2,1)S(1)}, u32[]{:S(2)}) copy-start(bf16[256,2048]{1,0:T(8,128)(2,1)S(1)} %get-tuple-element.27) | copy-start | bytes 3145732
  73.1 2.7 copy-start.13
  75.7 0.8 copy-start.3
  75.7 1.0 copy-start.16
  78.4 2.4 copy-start.4
  80.8 1.0 copy-start.12
  81.8 2.1 copy-start.9
  81.8 3.1 %copy-start.10 = (bf16[256,512]{0,1:T(8,128)(2,1)S(1)}, bf16[256,512]{0,1:T(8,128)(2,1)}, u32[]{:S(2)}) copy-start(bf16[256,512]{0,1:T(8,128)(2,1)} %copy.59) | copy-start | bytes 786436
  84.9 4.5 %copy-start.11 = (bf16[4,256,128]{1,2,0:T(8,128)(2,1)S(1)}, bf16[4,256,128]{1,2,0:T(8,128)(2,1)}, u32[]{:S(2)}) copy-start(bf16[4,256,128]{1,2,0:T(8,128)(2,1)} %fusion.33) | copy-start | bytes 786436
  90.3 2.7 copy-start.7
  112.1 6.2 %copy-start.2 = (bf16[256,512]{1,0:T(8,128)(2,1)S(1)}, bf16[256,512]{1,0:T(8,128)(2,1)}, u32[]{:S(2)}) copy-start(bf16[256,512]{1,0:T(8,128)(2,1)} %get-tuple-element.14) | copy-start | bytes 786436
  112.1 6.2 %copy-start.8 = (bf16[256,512]{1,0:T(8,128)(2,1)S(1)}, bf16[256,512]{1,0:T(8,128)(2,1)}, u32[]{:S(2)}) copy-start(bf16[256,512]{1,0:T(8,128)(2,1)} %param.17) | copy-start | bytes 786436
  114.9 59.6 %all-to-all-start.1 = ((bf16[32,32,512]{2,1,0:T(8,128)(2,1)}), bf16[32,32,512]{2,1,0:T(8,128)(2,1)}, u32[]{:S(2)}, u32[]{:S(2)}) async-start(bf16[32,32,512]{2,1,0:T(8,128)(2,1)} %bitcast.25), calls=%async_computation.1 | async-start | bytes 2097152 | tf_op jit(solution)/shard_map/all_to_all | solution.py:118
  118.3 165.0 %all-reduce.7.cloned.1.call-start = ((), (), s32[]{:S(2)}) async-start(), calls=%async_computation.2 | async-start | bytes 10485760 | tf_op jit(solution)/shard_map/psum | solution.py:114
  119.7 0.7 copy-start.14
  172.2 11.8 %copy-start.17 = (f32[512]{0:T(512)S(1)}, f32[512]{0:T(512)}, u32[]{:S(2)}) copy-start(f32[512]{0:T(512)} %param.10) | copy-start | bytes 6148
  172.2 12.4 %copy-start.1 = (f32[512,512]{1,0:T(8,128)S(1)}, f32[512,512]{1,0:T(8,128)}, u32[]{:S(2)}) copy-start(f32[512,512]{1,0:T(8,128)} %param.9) | copy-start | bytes 3145732
  283.3 5.0 %copy-start.6 = (f32[512,512]{1,0:T(8,128)S(1)}, f32[512,512]{1,0:T(8,128)}, u32[]{:S(2)}) copy-start(f32[512,512]{1,0:T(8,128)} %get-tuple-element.9) | copy-start | bytes 3145732
Sparse Core Ops, SparseCore 0:
  125.3 157.9 all-reduce.6
where the time goes:
time: 297 us; the launch traced here: 296 us
  waiting for transfers between devices  123 us (41%)
  blocking collectives  51.2 us (17%)
  other arithmetic  45.5 us (15%)
  local copies, waits for them, and re-layouts  31.9 us (11%)
  matrix products  19.7 us (7%)
  between operations  14.3 us (5%)
  starting transfers between devices  10.8 us (4%)
    psum x1, waiting for transfers between devices, body(): summed = lax.psum((grad_win, grad_wout, d_gain), ('grp', 'dev'))  96.3 us
    psum x1, blocking collectives, body(): summed = lax.psum((grad_win, grad_wout, d_gain), ('grp', 'dev'))  51.2 us
    all_to_all x1, waiting for transfers between devices, body(): lax.all_to_all(outgoing, ('grp', 'dev'), split_axis=0, concat_axis=0, til...  26.6 us
    gather x8, local copies, waits for them, and re-layouts, pool_rows(): received[token_slots[:, feature]].astype(jnp.float32)  14.8 us
    scatter-add x1, other arithmetic, presum(): jax.ops.segment_sum(spread.reshape(-1, d_pooled.shape[1]), token_slots.re...  14.6 us
    scatter-add x1, other arithmetic, body(): jax.ops.segment_sum(arriving.reshape(peer_count * slot_count, row_width),...  8.19 us
    dot_general x6, matrix products, narrow(): jnp.einsum(pattern, left_op, right_op, preferred_element_type=jnp.float32)  7.98 us
    all_to_all x1, starting transfers between devices, body(): lax.all_to_all(outgoing, ('grp', 'dev'), split_axis=0, concat_axis=0, til...  7.33 us
  transfers between devices with their start and end apart: 3, of which 2 were waited for; matrix products, arithmetic and copies ran while one was open for 6% of the time, Pallas kernels for 0%

commit v1 on v0

--- a/solution.py
+++ b/solution.py
@@ -4,9 +4,14 @@
 import jax
 import jax.numpy as jnp
 from jax import lax
+from jax.experimental import pallas as pl
+from jax.experimental.pallas import tpu as pltpu
 from jax.sharding import PartitionSpec as P
 
 HEADS = 4
+FAN = 4
+ROWS_FIRST = True
+ROTATE_NUM, ROTATE_DEN = 1, 4
 
 
 learn_rate = 0.2
@@ -49,20 +54,19 @@
     return (normed * norm_gain * gate_part.astype(jnp.float32)).astype(jnp.bfloat16)
 
 
-def pool_rows(received, token_slots):
-    pooled_sum = jnp.zeros((token_slots.shape[0], received.shape[1]), jnp.float32)
+def count_matrix(token_slots, slot_total):
+    slots = jnp.arange(slot_total, dtype=jnp.int32)
+    counts = jnp.zeros((token_slots.shape[0], slot_total), jnp.float32)
     for feature in range(token_slots.shape[1]):
-        pooled_sum = pooled_sum + received[token_slots[:, feature]].astype(jnp.float32)
-    return pooled_sum.astype(jnp.bfloat16)
-
-
-def presum(d_pooled, token_slots, slot_total):
-    spread = jnp.broadcast_to(
-        d_pooled[:, None, :], (token_slots.shape[0], token_slots.shape[1], d_pooled.shape[1])
-    )
-    return jax.ops.segment_sum(
-        spread.reshape(-1, d_pooled.shape[1]), token_slots.reshape(-1), num_segments=slot_total
-    )
+        counts = counts + (token_slots[:, feature : feature + 1] == slots[None, :]).astype(
+            jnp.float32
+        )
+    return counts.astype(jnp.bfloat16)
+
+
+def row_picker(row_lists, row_total):
+    rows = jnp.arange(row_total, dtype=jnp.int32)
+    return (row_lists.reshape(-1, 1) == rows[None, :]).astype(jnp.bfloat16)
 
 
 def dense_step(pooled, in_weight, out_weight, norm_gain, out_grad, seq_mask, head_count, product):
@@ -87,6 +91,217 @@
         jnp.float32
     )
     return (layer_out, grad_win, grad_wout, d_gain, d_pooled)
+
+
+def exchange_kernel(
+    peers,
+    dev_count,
+    levels,
+    row_ref,
+    gain_ref,
+    grad_ref,
+    arrive_ref,
+    gain_out,
+    full_ref,
+    *scratch,
+):
+    half_in, half_sum = scratch[0], scratch[1]
+    level_in = scratch[2 : 2 + levels]
+    level_sum = scratch[2 + levels : 2 + 2 * levels]
+    gains, row_send, row_recv, gain_send, gain_recv, tree_send, tree_recv = scratch[
+        2 + 2 * levels :
+    ]
+    grp = lax.axis_index("grp")
+    dev = lax.axis_index("dev")
+    me = grp * dev_count + dev
+    other = 1 - grp
+    barrier = pltpu.get_barrier_semaphore()
+
+    def place(step):
+        target = lax.rem(me + step, peers)
+        return (target // dev_count, lax.rem(target, dev_count))
+
+    def greet(step, carry):
+        pl.semaphore_signal(
+            barrier, inc=1, device_id=place(step), device_id_type=pl.DeviceIdType.MESH
+        )
+        return carry
+
+    lax.fori_loop(1, peers, greet, 0)
+    pl.semaphore_wait(barrier, peers - 1)
+
+    def tree_copy(index, source, landing, target):
+        return pltpu.make_async_remote_copy(
+            src_ref=source,
+            dst_ref=landing,
+            send_sem=tree_send.at[index],
+            recv_sem=tree_recv.at[index],
+            device_id=target,
+            device_id_type=pl.DeviceIdType.MESH,
+        )
+
+    half = peers // 2
+    first = tree_copy(0, grad_ref.at[pl.ds(other * half, half)], half_in, (other, dev))
+    first.start()
+
+    def row_copy(step):
+        target = lax.rem(me + step, peers)
+        return pltpu.make_async_remote_copy(
+            src_ref=row_ref.at[target],
+            dst_ref=arrive_ref.at[me],
+            send_sem=row_send.at[step],
+            recv_sem=row_recv.at[step],
+            device_id=place(step),
+            device_id_type=pl.DeviceIdType.MESH,
+        )
+
+    def row_landing(step):
+        source = lax.rem(me + peers - step, peers)
+        return pltpu.make_async_remote_copy(
+            src_ref=row_ref.at[source],
+            dst_ref=arrive_ref.at[source],
+            send_sem=row_send.at[step],
+            recv_sem=row_recv.at[step],
+            device_id=place(step),
+            device_id_type=pl.DeviceIdType.MESH,
+        )
+
+    def gain_copy(step):
+        return pltpu.make_async_remote_copy(
+            src_ref=gain_ref,
+            dst_ref=gains.at[step],
+            send_sem=gain_send.at[step],
+            recv_sem=gain_recv.at[step],
+            device_id=place(step),
+            device_id_type=pl.DeviceIdType.MESH,
+        )
+
+    def launch(i, carry):
+        step = 1 + lax.rem(i + ROTATE_NUM * peers // ROTATE_DEN, peers - 1)
+        row_copy(step).start()
+        gain_copy(step).start()
+        return carry
+
+    if ROWS_FIRST:
+        lax.fori_loop(0, peers - 1, launch, 0)
+    arrive_ref[me] = row_ref[me]
+    gains[0] = gain_ref[...]
+    first.wait()
+
+    def add_half(i, carry):
+        half_sum[i] = (
+            grad_ref[grp * half + i].astype(jnp.float32) + half_in[i].astype(jnp.float32)
+        ).astype(jnp.bfloat16)
+        return carry
+
+    lax.fori_loop(0, half, add_half, 0)
+    held, span, stride, slot = half_sum, half, 1, 1
+    base = grp * half
+    bases = []
+    for level in range(levels):
+        digit = lax.rem(dev // stride, FAN)
+        part = span // FAN
+        copies = []
+        for step in range(1, FAN):
+            there = lax.rem(digit + step, FAN)
+            target = (grp, dev + (there - digit) * stride)
+            copies.append(
+                tree_copy(
+                    slot, held.at[pl.ds(there * part, part)], level_in[level].at[step - 1], target
+                )
+            )
+            copies[-1].start()
+            slot += 1
+        if level == 0 and not ROWS_FIRST:
+            lax.fori_loop(0, peers - 1, launch, 0)
+        for copy in copies:
+            copy.wait()
+        final = level == levels - 1
+        base = base + digit * part
+
+        def add_level(i, carry, held=held, level=level, digit=digit, part=part, final=final, base=base):
+            total = held[digit * part + i].astype(jnp.float32)
+            for step in range(FAN - 1):
+                total = total + level_in[level][step, i].astype(jnp.float32)
+            if final:
+                full_ref[base + i] = total.astype(jnp.bfloat16)
+            else:
+                level_sum[level][i] = total.astype(jnp.bfloat16)
+            return carry
+
+        lax.fori_loop(0, part, add_level, 0)
+        bases.append((base, part, digit, stride))
+        held, span, stride = level_sum[level], part, stride * FAN
+    for base, part, digit, stride in reversed(bases):
+        copies = []
+        for step in range(1, FAN):
+            there = lax.rem(digit + step, FAN)
+            target = (grp, dev + (there - digit) * stride)
+            block = full_ref.at[pl.ds(base, part)]
+            copies.append((slot, step, tree_copy(slot, block, block, target)))
+            copies[-1][2].start()
+            slot += 1
+        for index, step, copy in copies:
+            copy.wait_send()
+            source = lax.rem(digit + FAN - step, FAN)
+            block = full_ref.at[pl.ds(base + (source - digit) * part, part)]
+            tree_copy(index, block, block, (grp, dev)).wait_recv()
+    mine = full_ref.at[pl.ds(grp * half, half)]
+    theirs = full_ref.at[pl.ds(other * half, half)]
+    last = tree_copy(slot, mine, mine, (other, dev))
+    last.start()
+
+    def finish(step, carry):
+        row_copy(step).wait_send()
+        row_landing(step).wait_recv()
+        gain_copy(step).wait()
+        return carry
+
+    lax.fori_loop(1, peers, finish, 0)
+    gain_out[...] = jnp.sum(gains[...], axis=0)
+    last.wait_send()
+    tree_copy(slot, theirs, theirs, (other, dev)).wait_recv()
+
+
+def exchange(row_grad, gain, grads):
+    peers, chunk, width = grads.shape
+    dev_count = lax.axis_size("dev")
+    levels, reach = 0, 1
+    while reach < dev_count:
+        levels, reach = levels + 1, reach * FAN
+    if reach != dev_count or peers != 2 * dev_count:
+        raise ValueError("unsupported mesh")
+    spans = [peers // 2 // FAN ** (k + 1) for k in range(levels)]
+    copies = 2 + 2 * (FAN - 1) * levels
+    low = jnp.bfloat16
+    vmem = pl.BlockSpec(memory_space=pltpu.VMEM)
+    return pl.pallas_call(
+        partial(exchange_kernel, peers, dev_count, levels),
+        out_shape=(
+            jax.ShapeDtypeStruct(row_grad.shape, row_grad.dtype),
+            jax.ShapeDtypeStruct(gain.shape, gain.dtype),
+            jax.ShapeDtypeStruct(grads.shape, grads.dtype),
+        ),
+        in_specs=[vmem] * 3,
+        out_specs=(vmem,) * 3,
+        scratch_shapes=[
+            pltpu.VMEM((peers // 2, chunk, width), low),
+            pltpu.VMEM((peers // 2, chunk, width), low),
+            *[pltpu.VMEM((FAN - 1, span, chunk, width), low) for span in spans],
+            *[pltpu.VMEM((span, chunk, width), low) for span in spans],
+            pltpu.VMEM((peers,) + gain.shape, jnp.float32),
+            pltpu.SemaphoreType.DMA((peers,)),
+            pltpu.SemaphoreType.DMA((peers,)),
+            pltpu.SemaphoreType.DMA((peers,)),
+            pltpu.SemaphoreType.DMA((peers,)),
+            pltpu.SemaphoreType.DMA((copies,)),
+            pltpu.SemaphoreType.DMA((copies,)),
+        ],
+        compiler_params=pltpu.CompilerParams(
+            collective_id=0, has_side_effects=True, vmem_limit_bytes=40 * 1024 * 1024
+        ),
+        name="exchange",
+    )(row_grad, gain, grads)
 
 
 def body(
@@ -103,25 +318,39 @@
     row_lists = send_rows[0]
     peer_count, slot_count = row_lists.shape
     row_width = emb_table.shape[1]
-    outgoing = emb_table[row_lists].astype(jnp.bfloat16)
+    picker = row_picker(row_lists, emb_table.shape[0])
+    outgoing = jnp.dot(
+        picker, emb_table.astype(jnp.bfloat16), preferred_element_type=jnp.float32
+    ).astype(jnp.bfloat16)
+    outgoing = outgoing.reshape(peer_count, slot_count, row_width)
     incoming = lax.all_to_all(outgoing, ("grp", "dev"), split_axis=0, concat_axis=0, tiled=True)
     received = incoming.reshape(peer_count * slot_count, row_width)
-    pooled = pool_rows(received, lookup_slot)
+    counts = count_matrix(lookup_slot, peer_count * slot_count)
+    pooled = jnp.dot(counts, received, preferred_element_type=jnp.float32).astype(jnp.bfloat16)
     seq_mask = build_mask(seq_lengths[0], lookup_slot.shape[0])
     layer_out, grad_win, grad_wout, d_gain, d_pooled = dense_step(
         pooled, in_weight, out_weight, norm_gain, out_grad, seq_mask, HEADS, narrow
     )
-    summed = lax.psum((grad_win, grad_wout, d_gain), ("grp", "dev"))
-    row_grad = presum(d_pooled, lookup_slot, peer_count * slot_count).reshape(
-        peer_count, slot_count, row_width
-    )
-    arriving = lax.all_to_all(
-        row_grad.astype(jnp.bfloat16), ("grp", "dev"), split_axis=0, concat_axis=0, tiled=True
-    ).astype(row_grad.dtype)
-    grad_rows = jax.ops.segment_sum(
+    row_grad = lax.dot_general(
+        counts,
+        d_pooled.astype(jnp.bfloat16),
+        (((0,), (0,)), ((), ())),
+        preferred_element_type=jnp.float32,
+    ).astype(jnp.bfloat16)
+    stacked = jnp.concatenate(
+        [part.astype(jnp.bfloat16) for part in jnp.split(grad_win, 4, axis=1) + [grad_wout]]
+    )
+    arriving, gain_sum, grad_sums = exchange(
+        row_grad.reshape(peer_count, slot_count, row_width),
+        d_gain[None, :],
+        stacked.reshape(peer_count, -1, row_width),
+    )
+    grad_blocks = grad_sums.reshape(5, row_width, row_width)
+    grad_rows = lax.dot_general(
+        picker,
         arriving.reshape(peer_count * slot_count, row_width),
-        row_lists.reshape(-1),
-        num_segments=emb_table.shape[0],
+        (((0,), (0,)), ((), ())),
+        preferred_element_type=jnp.float32,
     )
     state_new = adagrad_state + jnp.mean(grad_rows * grad_rows, axis=1)
     table_new = emb_table - learn_rate * grad_rows / (jnp.sqrt(state_new)[:, None] + adagrad_eps)
@@ -130,9 +359,9 @@
         layer_out,
         table_new,
         state_new,
-        summed[0] * grad_scale,
-        summed[1] * grad_scale,
-        summed[2] * grad_scale,
+        jnp.concatenate([grad_blocks[k].astype(jnp.float32) * grad_scale for k in range(4)], axis=1),
+        grad_blocks[4].astype(jnp.float32) * grad_scale,
+        gain_sum[0] * grad_scale,
     )
 
 

time: 297 us -> 149 us (0.50)
  waiting for transfers between devices: 123 us -> 25.6 us
  Pallas kernels: 0 us -> 65.1 us
  blocking collectives: 51.2 us -> 0 us
  other arithmetic: 45.5 us -> 14 us
  local copies, waits for them, and re-layouts: 31.9 us -> 9.34 us
  between operations: 14.3 us -> 0.97 us
  matrix products: 19.7 us -> 24.4 us
  starting transfers between devices: 10.8 us -> 7.46 us
    psum x1 -> x0, waiting for transfers between devices: 96.3 us -> none  [body(): summed = lax.psum((grad_win, grad_wout, d_gain), ('grp', 'dev'))]
    pallas_call x0 -> x1, Pallas kernels: none -> 65.1 us  [exchange(): pl.pallas_call(partial(exchange_kernel, peers, dev_count, levels), out_sh...]
    psum x1 -> x0, blocking collectives: 51.2 us -> none  [body(): summed = lax.psum((grad_win, grad_wout, d_gain), ('grp', 'dev'))]
    scatter-add x2 -> x0, other arithmetic: 22.8 us -> none  [the longest x1 14.6 us: presum(): jax.ops.segment_sum(spread.reshape(-1, d_pooled.shape[1]), token_slots.re...]
    gather x9 -> x0, local copies, waits for them, and re-layouts: 21.1 us -> none  [the longest x8 14.8 us: pool_rows(): received[token_slots[:, feature]].astype(jnp.float32)]
    dot_general x1 -> x4, matrix products: 1.54 us -> 9.74 us  [the longest x1 3.26 us: body(): lax.dot_general(counts, d_pooled.astype(jnp.bfloat16), (((0,), (0,)), (()...]
    convert_element_type x2 -> x0, other arithmetic: 4.53 us -> none  [the longest x1 2.75 us: body(): row_grad.astype(jnp.bfloat16)]
    unnamed x40 -> x43, local copies, waits for them, and re-layouts: 2.17 us -> 6.43 us
  transfers between devices with their start and end apart: 3 -> 1, of which waited for: 2 -> 1; matrix products, arithmetic and copies ran while one was open for 6% -> 2% of each run, Pallas kernels for 0% -> 0%
where the time goes in v1:
time: 149 us; the launch traced here: 147 us
  Pallas kernels  65.1 us (44%)
  waiting for transfers between devices  25.6 us (17%)
  matrix products  24.4 us (16%)
  other arithmetic  14 us (9%)
  local copies, waits for them, and re-layouts  9.34 us (6%)
  starting transfers between devices  7.46 us (5%)
    pallas_call x1, Pallas kernels, exchange(): pl.pallas_call(partial(exchange_kernel, peers, dev_count, levels), out_sh...  65.1 us
    all_to_all x1, waiting for transfers between devices, body(): lax.all_to_all(outgoing, ('grp', 'dev'), split_axis=0, concat_axis=0, til...  25.6 us
    all_to_all x1, starting transfers between devices, body(): lax.all_to_all(outgoing, ('grp', 'dev'), split_axis=0, concat_axis=0, til...  7.46 us
    dot_general x6, matrix products, narrow(): jnp.einsum(pattern, left_op, right_op, preferred_element_type=jnp.float32)  7.44 us
    unnamed x43, local copies, waits for them, and re-layouts  6.43 us
    convert_element_type x1, other arithmetic, dense_step(): d_low = d_preact.astype(jnp.bfloat16)  3.44 us
    mul x1, other arithmetic, body(): grad_blocks[4].astype(jnp.float32) * grad_scale  3.39 us
    dot_general x1, matrix products, body(): lax.dot_general(counts, d_pooled.astype(jnp.bfloat16), (((0,), (0,)), (()...  3.26 us
  transfers between devices with their start and end apart: 1, of which 1 were waited for; matrix products, arithmetic and copies ran while one was open for 2% of the time, Pallas kernels for 0%

profile of v1, /device:TPU:0, one launch (start us, length us, event | category | flops | bytes accessed | tf_op | source)
XLA Modules:
  0.0 146.8 jit_solution(16821308170263087792)
XLA Ops:
  0.6 0.0 copy-start
  0.6 0.9 eq.184
  1.6 3.0 %fusion.5 = bf16[1024,512]{1,0:T(8,128)(2,1)} fusion(s32[1024]{0:T(1024)S(1)} %eq.184, f32[512,512]{1,0:T(8,128)} %param.9), kind=kOutput, calls=%fused_computation.14 | convolution fusion | flops 538181632 | bytes 2101248 | tf_op jit(solution)/shard_map/dot_general | solution.py:322
  4.6 7.5 %all-to-all-start = ((bf16[32,32,512]{2,1,0:T(8,128)(2,1)}), bf16[32,32,512]{2,1,0:T(8,128)(2,1)}, u32[]{:S(2)}, u32[]{:S(2)}) async-start(bf16[32,32,512]{2,1,0:T(8,128)(2,1)} %bitcast.89), calls=%async_computation | async-start | bytes 2097152 | tf_op jit(solution)/shard_map/all_to_all | solution.py:326
  12.1 1.3 copy.41
  13.4 0.2 reduce-window.8
  13.6 0.1 fusion.29
  13.7 0.8 fusion.26
  14.5 25.6 %all-to-all-done = bf16[32,32,512]{2,1,0:T(8,128)(2,1)} async-done(((bf16[32,32,512]{2,1,0:T(8,128)(2,1)}), bf16[32,32,512]{2,1,0:T(8,128)(2,1)}, u32[]{:S(2)}, u32[]{:S(2)}) %all-to-all-start) | async-done | bytes 1048608 | tf_op jit(solution)/shard_map/all_to_all | solution.py:326
  40.1 2.5 %convolution_convert_fusion.7 = bf16[256,512]{1,0:T(8,128)(2,1)S(1)} fusion(bf16[1024,512]{1,0:T(8,128)(2,1)} %bitcast.9, s32[256]{0:T(256)S(1)} %bitcast.112, s32[256]{0:T(256)S(1)} %bitcast.114, s32[256]{0:T(256)S(1)} %bitcast.102, s32[256]{0:T(256)S(1)} %bitcast.104, s32[256]{0:T(256)S(1)} %bitcast.106, s32[256]{0:T(256)S(1)} %bitcast.108, ...), kind=kOutput, calls=%fused_computation.30 | convolution fusion | flops 274857984 | bytes 1318912 | tf_op jit(solution)/shard_map/dot_general | solution.py:329
  42.6 2.1 %multiply_convert_fusion = (bf16[256,2048]{1,0:T(8,128)(2,1)S(1)}, f32[256,2048]{1,0:T(8,128)}) fusion(bf16[256,512]{1,0:T(8,128)(2,1)S(1)} %convolution_convert_fusion.7, bf16[512,2048]{1,0:T(8,128)(2,1)S(1)} %copy-done), kind=kOutput, calls=%fused_computation.8 | convolution fusion | flops 539492352 | bytes 5505024 | tf_op jit(solution)/shard_map/dot_general | solution.py:73
  44.7 1.0 copy-done.5
  45.7 0.1 slice_bitcast_fusion
  45.7 0.1 copy.50
  45.9 0.1 copy.49
  46.0 2.6 %multiply_convert_fusion.1 = (bf16[4,256,256]{2,1,0:T(8,128)(2,1)S(1)}, f32[4,256,256]{2,1,0:T(8,128)}) fusion(f32[256,256]{1,0:T(8,128)} %fusion.26, bf16[256,4,128]{0,2,1:T(8,128)(2,1)S(1)} %bitcast.92, bf16[256,4,128]{0,2,1:T(8,128)(2,1)S(1)} %bitcast.90), kind=kOutput, calls=%fused_computation.42 | convolution fusion | flops 68943872 | bytes 2359296 | tf_op jit(solution)/shard_map/jvp(thd,shd->hts)/dot_general | solution.py:23
  48.6 0.3 fusion.33
  49.0 0.1 fusion.19
  49.1 0.3 copy-done.4
  49.4 0.2 copy.44
  49.6 1.7 %multiply_reduce_fusion.1 = (f32[512]{0:T(512)S(1)}, f32[256]{0:T(256)S(1)}, f32[256,512]{1,0:T(8,128)S(1)}) fusion(f32[256,512]{1,0:T(8,128)S(1)} %copy.44, f32[256]{0:T(256)S(1)} %fusion.30, f32[256]{0:T(256)S(1)} %broadcast_multiply_fusion.1, bf16[256,2048]{1,0:T(8,128)(2,1)} %copy-done.5, f32[512]{0:T(512)S(1)} %copy-done.15, ...), kind=kOutput, calls=%fused_computation.66 | convolution fusion | flops 135658752 | bytes 2104320 | tf_op jit(solution)/shard_map/dot_general | solution.py:84
  51.3 2.1 %fusion.31 = (f32[256]{0:T(256)S(1)}, f32[256,512]{1,0:T(8,128)S(1)}, bf16[256,512]{1,0:T(8,128)(2,1)}, bf16[256,512]{1,0:T(8,128)(2,1)}) fusion(f32[256]{0:T(256)S(1)} %multiply_multiply_fusion, f32[256,512]{1,0:T(8,128)S(1)} %copy.44, f32[256]{0:T(256)S(1)} %broadcast_multiply_fusion.1, f32[256]{0:T(256)S(1)} %fusion.30, f32[512]{0:T(512)S(1)} %copy-done.15, ...), kind=kLoop, calls=%fused_computation.91 | loop fusion | flops 1965824 | bytes 2365440 | tf_op jit(solution)/shard_map/transpose(jvp())/reduce_sum | solution.py:51
  53.4 0.1 broadcast_add_fusion
  53.5 0.1 copy.45
  53.6 1.3 fusion.36
  54.9 2.0 %fusion.14 = bf16[4,256,256]{2,1,0:T(8,128)(2,1)S(1)} fusion(f32[4,256,256]{2,1,0:T(8,128)} %get-tuple-element.51, bf16[4,128,256]{2,1,0:T(8,128)(2,1)S(1)} %bitcast.97, f32[256,256]{1,0:T(8,128)} %fusion.26, bf16[32,4,8,128]{3,2,1,0:T(8,128)(2,1)} %copy-done.12), kind=kOutput, calls=%fused_computation.34 | convolution fusion | flops 70516736 | bytes 2359296 | tf_op jit(solution)/shard_map/transpose(jvp(hts,shd->thd))/dot_general | solution.py:23
  57.0 0.3 fusion.34
  57.3 0.9 fusion.35
  58.2 0.1 copy.48
  58.4 1.1 copy.46
  59.5 0.1 copy.47
  59.6 3.4 %fusion.1 = bf16[256,2048]{1,0:T(8,128)(2,1)} fusion(f32[256,2048]{1,0:T(8,128)} %get-tuple-element.49, bf16[256,512]{1,0:T(8,128)(2,1)} %get-tuple-element.36, bf16[256,512]{1,0:T(8,128)(2,1)S(1)} %copy.48, bf16[256,512]{1,0:T(8,128)(2,1)S(1)} %copy.47, bf16[256,512]{1,0:T(8,128)(2,1)S(1)} %copy.46), kind=kLoop, calls=%fused_computation.6 | loop fusion | flops 9437184 | bytes 4194304 | tf_op jit(solution)/shard_map/convert_element_type | solution.py:88
  63.1 3.3 %convolution_convert_fusion.1 = bf16[1024,512]{1,0:T(8,128)(2,1)S(1)} fusion(bf16[256,2048]{1,0:T(8,128)(2,1)} %fusion.1, bf16[512,2048]{1,0:T(8,128)(2,1)S(1)} %copy-done, bf16[256,512]{1,0:T(8,128)(2,1)} %param.17, s32[256]{0:T(256)S(1)} %bitcast.113, s32[256]{0:T(256)S(1)} %bitcast.115, s32[256]{0:T(256)S(1)} %bitcast.103, s32[256]{0:T(256)S(1)} %bitcast.105, ...), kind=kOutput, calls=%fused_computation.15 | convolution fusion | flops 812515328 | bytes 4464640 | tf_op jit(solution)/shard_map/dot_general | solution.py:334
  66.3 0.0 copy-start.3
  66.4 2.0 %convolution_convert_fusion = bf16[512,2048]{1,0:T(8,128)(2,1)S(1)} fusion(bf16[256,512]{1,0:T(8,128)(2,1)S(1)} %convolution_convert_fusion.7, bf16[256,2048]{1,0:T(8,128)(2,1)} %fusion.1), kind=kOutput, calls=%fused_computation.2 | convolution fusion | flops 537919488 | bytes 3407872 | tf_op jit(solution)/shard_map/dot_general | solution.py:89
  68.4 1.0 fusion.10
  69.6 0.8 copy-done.13
  70.4 0.3 fusion.6
  70.7 65.1 %exchange.1 = (bf16[32,32,512]{2,1,0:T(8,128)(2,1)S(1)}, f32[1,512]{1,0:T(1,128)S(1)}, bf16[32,80,512]{2,1,0:T(8,128)(2,1)S(1)}) custom-call(bf16[32,32,512]{2,1,0:T(8,128)(2,1)S(1)} %bitcast.85, f32[1,512]{1,0:T(1,128)S(1)} %bitcast.86, bf16[32,80,512]{2,1,0:T(8,128)(2,1)S(1)} %bitcast.83), custom_call_target="tpu_custom_call" | custom-call | tf_op jit(solution)/shard_map/exchange/pallas_call | solution.py:278
  135.8 0.0 copy-start.1
  135.8 1.5 %copy-done.1 = bf16[32,80,512]{2,1,0:T(8,128)(2,1)} copy-done((bf16[32,80,512]{2,1,0:T(8,128)(2,1)}, bf16[32,80,512]{2,1,0:T(8,128)(2,1)S(1)}, u32[]{:S(2)}) %copy-start.1) | copy-done | bytes 2621464
  137.3 1.0 multiply_reduce_fusion
  138.3 0.6 broadcast_multiply_fusion
  138.9 0.6 sqrt_add_fusion
  139.5 0.2 divide_subtract_fusion
  139.7 1.3 copy.42
  141.0 3.4 %multiply_bitcast_fusion = (f32[512,512]{1,0:T(8,128)}, f32[512,512]{1,0:T(8,128)S(1)}, f32[512,512]{1,0:T(8,128)S(1)}, f32[512,512]{1,0:T(8,128)S(1)}, f32[512,512]{1,0:T(8,128)S(1)}) fusion(bf16[5,512,512]{2,1,0:T(8,128)(2,1)} %bitcast.84), kind=kLoop, calls=%fused_computation.35 | loop fusion | flops 2621440 | bytes 7864320 | tf_op jit(solution)/shard_map/mul | solution.py:363
  144.4 2.4 %pad_maximum_fusion = f32[512,2048]{1,0:T(8,128)} fusion(f32[512,512]{1,0:T(8,128)S(1)} %get-tuple-element.31, f32[512,512]{1,0:T(8,128)S(1)} %get-tuple-element.32, f32[512,512]{1,0:T(8,128)S(1)} %get-tuple-element.33, f32[512,512]{1,0:T(8,128)S(1)} %get-tuple-element.34), kind=kLoop, calls=%fused_computation | loop fusion | flops 3145728 | bytes 8388608 | tf_op jit(solution)/shard_map/concatenate | solution.py:362
  (38 shorter events, 0.2 us)
Async XLA Ops:
  0.6 41.9 %copy-start = (bf16[512,2048]{1,0:T(8,128)(2,1)S(1)}, bf16[512,2048]{1,0:T(8,128)(2,1)}, u32[]{:S(2)}) copy-start(bf16[512,2048]{1,0:T(8,128)(2,1)} %param.14) | copy-start | bytes 6291460
  1.6 10.5 %copy-start.6 = (f32[512,512]{1,0:T(8,128)S(1)}, f32[512,512]{1,0:T(8,128)}, u32[]{:S(2)}) copy-start(f32[512,512]{1,0:T(8,128)} %param.9) | copy-start | bytes 3145732
  4.6 8.8 %copy-start.17 = (s32[1,2]{1,0:T(1,128)S(1)}, s32[1,2]{1,0:T(1,128)}, u32[]{:S(2)}) copy-start(s32[1,2]{1,0:T(1,128)} %param.13) | copy-start | bytes 28
  4.6 9.0 %copy-start.14 = (s32[256,8]{0,1:T(8,128)S(1)}, s32[256,8]{0,1:T(8,128)}, u32[]{:S(2)}) copy-start(s32[256,8]{0,1:T(8,128)} %param.12) | copy-start | bytes 24580
  4.6 35.5 %all-to-all-start = ((bf16[32,32,512]{2,1,0:T(8,128)(2,1)}), bf16[32,32,512]{2,1,0:T(8,128)(2,1)}, u32[]{:S(2)}, u32[]{:S(2)}) async-start(bf16[32,32,512]{2,1,0:T(8,128)(2,1)} %bitcast.89), calls=%async_computation | async-start | bytes 2097152 | tf_op jit(solution)/shard_map/all_to_all | solution.py:326
  44.7 1.0 copy-start.5
  45.7 2.9 %copy-start.12 = (bf16[32,4,8,128]{3,2,1,0:T(8,128)(2,1)}, bf16[32,4,8,128]{3,2,1,0:T(8,128)(2,1)S(1)}, u32[]{:S(2)}) copy-start(bf16[32,4,8,128]{3,2,1,0:T(8,128)(2,1)S(1)} %get-tuple-element.37) | copy-start | bytes 786436
  45.9 2.7 %copy-start.7 = (bf16[256,512]{0,1:T(8,128)(2,1)}, bf16[256,512]{0,1:T(8,128)(2,1)S(1)}, u32[]{:S(2)}) copy-start(bf16[256,512]{0,1:T(8,128)(2,1)S(1)} %copy.50) | copy-start | bytes 786436
  46.0 2.6 %copy-start.9 = (bf16[256,512]{0,1:T(8,128)(2,1)}, bf16[256,512]{0,1:T(8,128)(2,1)S(1)}, u32[]{:S(2)}) copy-start(bf16[256,512]{0,1:T(8,128)(2,1)S(1)} %copy.49) | copy-start | bytes 786436
  48.6 0.8 copy-start.4
  48.6 1.0 copy-start.15
  54.9 2.0 %copy-start.8 = (bf16[256,512]{0,1:T(8,128)(2,1)S(1)}, bf16[256,512]{0,1:T(8,128)(2,1)}, u32[]{:S(2)}) copy-start(bf16[256,512]{0,1:T(8,128)(2,1)} %copy-done.7) | copy-start | bytes 786436
  54.9 2.4 %copy-start.10 = (bf16[256,512]{0,1:T(8,128)(2,1)S(1)}, bf16[256,512]{0,1:T(8,128)(2,1)}, u32[]{:S(2)}) copy-start(bf16[256,512]{0,1:T(8,128)(2,1)} %copy-done.9) | copy-start | bytes 786436
  66.3 2.1 %copy-start.3 = (bf16[512,512]{1,0:T(8,128)(2,1)S(1)}, bf16[512,512]{1,0:T(8,128)(2,1)}, u32[]{:S(2)}) copy-start(bf16[512,512]{1,0:T(8,128)(2,1)} %param.15) | copy-start | bytes 1572868
  66.3 2.1 %copy-start.11 = (bf16[256,512]{1,0:T(8,128)(2,1)S(1)}, bf16[256,512]{1,0:T(8,128)(2,1)}, u32[]{:S(2)}) copy-start(bf16[256,512]{1,0:T(8,128)(2,1)} %get-tuple-element.35) | copy-start | bytes 786436
  69.4 0.9 copy-start.13
  135.8 1.5 %copy-start.1 = (bf16[32,80,512]{2,1,0:T(8,128)(2,1)}, bf16[32,80,512]{2,1,0:T(8,128)(2,1)S(1)}, u32[]{:S(2)}) copy-start(bf16[32,80,512]{2,1,0:T(8,128)(2,1)S(1)} %get-tuple-element.10) | copy-start | bytes 7864324
  137.3 1.6 %copy-start.16 = (f32[512]{0:T(512)S(1)}, f32[512]{0:T(512)}, u32[]{:S(2)}) copy-start(f32[512]{0:T(512)} %param.10) | copy-start | bytes 6148
  137.3 2.2 %copy-start.2 = (f32[512,512]{0,1:T(8,128)S(1)}, f32[512,512]{0,1:T(8,128)}, u32[]{:S(2)}) copy-start(f32[512,512]{0,1:T(8,128)} %copy.41) | copy-start | bytes 3145732

commit v2 on v1

--- a/solution.py
+++ b/solution.py
@@ -19,10 +19,6 @@
 adagrad_eps = 1e-08
 
 
-def narrow(pattern, left_op, right_op):
-    return jnp.einsum(pattern, left_op, right_op, preferred_element_type=jnp.float32)
-
-
 def build_mask(lengths, slot_total):
     positions = jnp.arange(slot_total, dtype=jnp.int32)
     bounds = jnp.cumsum(lengths, dtype=jnp.int32)
@@ -32,26 +28,6 @@
     same_seq = sequence_id[:, None] == sequence_id[None, :]
     causal = positions[None, :] <= positions[:, None]
     return (same_seq & causal).astype(jnp.float32)
-
-
-def attend(preact, norm_gain, seq_mask, head_count, product):
-    activated = jax.nn.silu(preact).astype(jnp.bfloat16)
-    tokens_here, stacked = activated.shape
-    model_width = stacked // 4
-    head_dim = model_width // head_count
-    gate_part = activated[:, :model_width]
-    values = activated[:, model_width : 2 * model_width].reshape(tokens_here, head_count, head_dim)
-    queries = activated[:, 2 * model_width : 3 * model_width].reshape(
-        tokens_here, head_count, head_dim
-    )
-    keys_all = activated[:, 3 * model_width :].reshape(tokens_here, head_count, head_dim)
-    scores = product("thd,shd->hts", queries, keys_all) * (1.0 / math.sqrt(head_dim))
-    weights = (jax.nn.silu(scores) * seq_mask).astype(jnp.bfloat16)
-    attended = product("hts,shd->thd", weights, values).reshape(tokens_here, model_width)
-    center = attended - jnp.mean(attended, axis=1, keepdims=True)
-    spread = jnp.mean(center * center, axis=1, keepdims=True)
-    normed = center * lax.rsqrt(spread + norm_eps)
-    return (normed * norm_gain * gate_part.astype(jnp.float32)).astype(jnp.bfloat16)
 
 
 def count_matrix(token_slots, slot_total):
@@ -64,33 +40,137 @@
     return counts.astype(jnp.bfloat16)
 
 
+def spread_matrix(token_slots, slot_total):
+    slots = jnp.arange(slot_total, dtype=jnp.int32)
+    across = token_slots.T
+    counts = jnp.zeros((slot_total, token_slots.shape[0]), jnp.float32)
+    for feature in range(token_slots.shape[1]):
+        counts = counts + (slots[:, None] == across[feature : feature + 1]).astype(jnp.float32)
+    return counts.astype(jnp.bfloat16)
+
+
 def row_picker(row_lists, row_total):
     rows = jnp.arange(row_total, dtype=jnp.int32)
     return (row_lists.reshape(-1, 1) == rows[None, :]).astype(jnp.bfloat16)
 
 
-def dense_step(pooled, in_weight, out_weight, norm_gain, out_grad, seq_mask, head_count, product):
-    preact = jnp.dot(pooled, in_weight, preferred_element_type=jnp.float32)
-    mixed_out, pullback = jax.vjp(
-        partial(attend, seq_mask=seq_mask, head_count=head_count, product=product),
-        preact,
-        norm_gain,
-    )
-    layer_out = (
-        jnp.dot(mixed_out, out_weight, preferred_element_type=jnp.float32)
-        + pooled.astype(jnp.float32)
-    ).astype(jnp.bfloat16)
-    grad_wout = jnp.dot(mixed_out.T, out_grad, preferred_element_type=jnp.float32)
-    d_mixed = jnp.dot(out_grad, out_weight.T, preferred_element_type=jnp.float32).astype(
-        jnp.bfloat16
-    )
-    d_preact, d_gain = pullback(d_mixed)
-    d_low = d_preact.astype(jnp.bfloat16)
-    grad_win = jnp.dot(pooled.T, d_low, preferred_element_type=jnp.float32)
-    d_pooled = jnp.dot(d_low, in_weight.T, preferred_element_type=jnp.float32) + out_grad.astype(
-        jnp.float32
-    )
-    return (layer_out, grad_win, grad_wout, d_gain, d_pooled)
+def mul(left_op, right_op, left_dim, right_dim):
+    return lax.dot_general(
+        left_op,
+        right_op,
+        (((left_dim,), (right_dim,)), ((), ())),
+        preferred_element_type=jnp.float32,
+    )
+
+
+def layer_kernel(
+    counts_ref,
+    spread_ref,
+    received_ref,
+    win_ref,
+    wout_ref,
+    gain_ref,
+    cot_ref,
+    dmixed_ref,
+    mask_ref,
+    layer_ref,
+    grads_ref,
+    dgain_ref,
+    row_ref,
+    slope_ref,
+    low_ref,
+):
+    low = jnp.bfloat16
+    width = cot_ref.shape[1]
+    head_dim = width // HEADS
+    scale = 1.0 / math.sqrt(head_dim)
+    pooled = mul(counts_ref[...], received_ref[...], 1, 0).astype(low)
+    active = []
+    for block in range(4):
+        columns = pl.ds(block * width, width)
+        preact = mul(pooled, win_ref[:, columns], 1, 0)
+        gate = jax.nn.sigmoid(preact)
+        active.append((preact * gate).astype(low))
+        slope_ref[:, columns] = gate * (1.0 + preact * (1.0 - gate))
+    gate_part, values, queries, keys_all = active
+    gate_part = gate_part.astype(jnp.float32)
+    mask = mask_ref[...]
+    weights, slopes, parts = [], [], []
+    for head in range(HEADS):
+        cut = slice(head * head_dim, (head + 1) * head_dim)
+        scores = mul(queries[:, cut], keys_all[:, cut], 1, 1) * scale
+        gate = jax.nn.sigmoid(scores)
+        weights.append((scores * gate * mask).astype(low))
+        slopes.append(gate * (1.0 + scores * (1.0 - gate)) * mask)
+        parts.append(mul(weights[-1], values[:, cut], 1, 0))
+    attended = jnp.concatenate(parts, axis=1)
+    center = attended - jnp.mean(attended, axis=1, keepdims=True)
+    spread = jnp.mean(center * center, axis=1, keepdims=True)
+    inverse = lax.rsqrt(spread + norm_eps)
+    normed = center * inverse
+    gain = gain_ref[...]
+    mixed = (normed * gain * gate_part).astype(low)
+    layer_ref[...] = (mul(mixed, wout_ref[...], 1, 0) + pooled.astype(jnp.float32)).astype(low)
+    grads_ref[pl.ds(4 * width, width), :] = mul(mixed, cot_ref[...], 0, 0).astype(low)
+    d_mixed = dmixed_ref[...].astype(jnp.float32)
+    dgain_ref[...] = jnp.sum(d_mixed * normed * gate_part, axis=0, keepdims=True)
+    d_gate = (d_mixed * (normed * gain)).astype(low)
+    low_ref[:, pl.ds(0, width)] = (
+        d_gate.astype(jnp.float32) * slope_ref[:, pl.ds(0, width)]
+    ).astype(low)
+    d_normed = d_mixed * gate_part * gain
+    d_attended = inverse * (
+        d_normed
+        - jnp.mean(d_normed, axis=1, keepdims=True)
+        - normed * jnp.mean(d_normed * normed, axis=1, keepdims=True)
+    )
+    d_attended = d_attended.astype(low)
+    for head in range(HEADS):
+        cut = slice(head * head_dim, (head + 1) * head_dim)
+        d_part = d_attended[:, cut]
+        d_weights = mul(d_part, values[:, cut], 1, 1).astype(low)
+        d_scores = (d_weights.astype(jnp.float32) * slopes[head] * scale).astype(low)
+        for block, grad in (
+            (1, mul(weights[head], d_part, 0, 0)),
+            (2, mul(d_scores, keys_all[:, cut], 1, 0)),
+            (3, mul(d_scores, queries[:, cut], 0, 0)),
+        ):
+            columns = pl.ds(block * width + head * head_dim, head_dim)
+            low_ref[:, columns] = (
+                grad.astype(low).astype(jnp.float32) * slope_ref[:, columns]
+            ).astype(low)
+    d_low = low_ref[...]
+    d_pooled = mul(d_low, win_ref[...], 1, 1) + cot_ref[...].astype(jnp.float32)
+    row_ref[...] = mul(spread_ref[...], d_pooled.astype(low), 1, 0).astype(low)
+    grad_win = mul(pooled, d_low, 0, 0).astype(low)
+    for block in range(4):
+        grads_ref[pl.ds(block * width, width), :] = grad_win[:, block * width : (block + 1) * width]
+
+
+def layer(counts, spread, received, in_weight, out_weight, norm_gain, out_grad, d_mixed, seq_mask):
+    tokens, width = out_grad.shape
+    low = jnp.bfloat16
+    vmem = pl.BlockSpec(memory_space=pltpu.VMEM)
+    return pl.pallas_call(
+        layer_kernel,
+        out_shape=(
+            jax.ShapeDtypeStruct((tokens, width), low),
+            jax.ShapeDtypeStruct((5 * width, width), low),
+            jax.ShapeDtypeStruct((1, width), jnp.float32),
+            jax.ShapeDtypeStruct((spread.shape[0], width), low),
+        ),
+        in_specs=[vmem] * 9,
+        out_specs=(vmem,) * 4,
+        scratch_shapes=[
+            pltpu.VMEM((tokens, 4 * width), jnp.float32),
+            pltpu.VMEM((tokens, 4 * width), low),
+        ],
+        cost_estimate=pl.CostEstimate(
+            flops=26 * tokens * width * width, bytes_accessed=1 << 23, transcendentals=1 << 20
+        ),
+        compiler_params=pltpu.CompilerParams(vmem_limit_bytes=40 * 1024 * 1024),
+        name="layer",
+    )(counts, spread, received, in_weight, out_weight, norm_gain, out_grad, d_mixed, seq_mask)
 
 
 def exchange_kernel(
@@ -326,24 +406,26 @@
     incoming = lax.all_to_all(outgoing, ("grp", "dev"), split_axis=0, concat_axis=0, tiled=True)
     received = incoming.reshape(peer_count * slot_count, row_width)
     counts = count_matrix(lookup_slot, peer_count * slot_count)
-    pooled = jnp.dot(counts, received, preferred_element_type=jnp.float32).astype(jnp.bfloat16)
+    spread = spread_matrix(lookup_slot, peer_count * slot_count)
     seq_mask = build_mask(seq_lengths[0], lookup_slot.shape[0])
-    layer_out, grad_win, grad_wout, d_gain, d_pooled = dense_step(
-        pooled, in_weight, out_weight, norm_gain, out_grad, seq_mask, HEADS, narrow
-    )
-    row_grad = lax.dot_general(
+    d_mixed = jnp.dot(out_grad, out_weight.T, preferred_element_type=jnp.float32).astype(
+        jnp.bfloat16
+    )
+    layer_out, grads, d_gain, row_grad = layer(
         counts,
-        d_pooled.astype(jnp.bfloat16),
-        (((0,), (0,)), ((), ())),
-        preferred_element_type=jnp.float32,
-    ).astype(jnp.bfloat16)
-    stacked = jnp.concatenate(
-        [part.astype(jnp.bfloat16) for part in jnp.split(grad_win, 4, axis=1) + [grad_wout]]
+        spread,
+        received,
+        in_weight,
+        out_weight,
+        norm_gain[None, :],
+        out_grad,
+        d_mixed,
+        seq_mask,
     )
     arriving, gain_sum, grad_sums = exchange(
         row_grad.reshape(peer_count, slot_count, row_width),
-        d_gain[None, :],
-        stacked.reshape(peer_count, -1, row_width),
+        d_gain,
+        grads.reshape(peer_count, -1, row_width),
     )
     grad_blocks = grad_sums.reshape(5, row_width, row_width)
     grad_rows = lax.dot_general(

time: 149 us -> 123 us (0.83)
  matrix products: 24.4 us -> 4.28 us
  Pallas kernels: 65.1 us -> 70.2 us
  other arithmetic: 14 us -> 9.09 us
  local copies, waits for them, and re-layouts: 9.34 us -> 6.36 us
  waiting for transfers between devices: 25.6 us -> 23.7 us
    dot_general x13 -> x1, matrix products: 20.3 us -> 0.33 us  [body(): jnp.dot(out_grad, out_weight.T, preferred_element_type=jnp.float32)]
    pallas_call x0 -> x1, Pallas kernels: none -> 5.11 us  [layer(): pl.pallas_call(layer_kernel, out_shape=(jax.ShapeDtypeStruct((tokens, wid...]
    reduce_sum x2 -> x0, other arithmetic: 2.16 us -> none  [the longest x1 2.05 us: attend(): center = attended - jnp.mean(attended, axis=1, keepdims=True)]
    reshape x7 -> x0, local copies, waits for them, and re-layouts: 1.96 us -> none  [the longest x2 1.22 us: attend(): activated[:, 3 * model_width:].reshape(tokens_here, head_count, head_dim)]
    all_to_all x1, waiting for transfers between devices: 25.6 us -> 23.7 us  [body(): lax.all_to_all(outgoing, ('grp', 'dev'), split_axis=0, concat_axis=0, til...]
    mul x1, other arithmetic: 3.39 us -> 1.71 us  [body(): grad_blocks[4].astype(jnp.float32) * grad_scale]
    convert_element_type x1 -> x2, other arithmetic: 3.44 us -> 2.24 us  [the longest x1 1.2 us: count_matrix(): return counts.astype(jnp.bfloat16)]
    unnamed x43 -> x20, local copies, waits for them, and re-layouts: 6.43 us -> 5.47 us
  transfers between devices with their start and end apart: 1 -> 1, of which waited for: 1 -> 1; matrix products, arithmetic and copies ran while one was open for 2% -> 3% of each run, Pallas kernels for 0% -> 0%
where the time goes in v2:
time: 123 us; the launch traced here: 122 us
  Pallas kernels  70.2 us (57%)
  waiting for transfers between devices  23.7 us (19%)
  other arithmetic  9.09 us (7%)
  starting transfers between devices  7.33 us (6%)
  local copies, waits for them, and re-layouts  6.36 us (5%)
  matrix products  4.28 us (3%)
    pallas_call x1, Pallas kernels, exchange(): pl.pallas_call(partial(exchange_kernel, peers, dev_count, levels), out_sh...  65.1 us
    all_to_all x1, waiting for transfers between devices, body(): lax.all_to_all(outgoing, ('grp', 'dev'), split_axis=0, concat_axis=0, til...  23.7 us
    all_to_all x1, starting transfers between devices, body(): lax.all_to_all(outgoing, ('grp', 'dev'), split_axis=0, concat_axis=0, til...  7.33 us
    unnamed x20, local copies, waits for them, and re-layouts  5.47 us
    pallas_call x1, Pallas kernels, layer(): pl.pallas_call(layer_kernel, out_shape=(jax.ShapeDtypeStruct((tokens, wid...  5.11 us
    dot_general x1, matrix products, body(): jnp.dot(picker, emb_table.astype(jnp.bfloat16), preferred_element_type=jn...  2.95 us
  transfers between devices with their start and end apart: 1, of which 1 were waited for; matrix products, arithmetic and copies ran while one was open for 3% of the time, Pallas kernels for 0%

profile of v2, /device:TPU:0, one launch (start us, length us, event | category | flops | bytes accessed | tf_op | source)
XLA Modules:
  0.0 121.7 jit_solution(10581678900696510229)
XLA Ops:
  0.6 0.0 copy-start.5
  0.6 0.9 eq.332
  1.5 3.0 %fusion.2 = bf16[1024,512]{1,0:T(8,128)(2,1)} fusion(s32[1024]{0:T(1024)S(1)} %eq.332, f32[512,512]{1,0:T(8,128)} %param.9), kind=kOutput, calls=%fused_computation.4 | convolution fusion | flops 538181632 | bytes 2101248 | tf_op jit(solution)/shard_map/dot_general | solution.py:402
  4.5 0.0 copy-start.8
  4.5 0.0 copy-start.6
  4.5 0.0 copy-start
  4.5 0.0 copy-start.1
  4.5 7.3 %all-to-all-start = ((bf16[32,32,512]{2,1,0:T(8,128)(2,1)}), bf16[32,32,512]{2,1,0:T(8,128)(2,1)S(1)}, u32[]{:S(2)}, u32[]{:S(2)}) async-start(bf16[32,32,512]{2,1,0:T(8,128)(2,1)} %bitcast.46), calls=%async_computation | async-start | bytes 2097152 | tf_op jit(solution)/shard_map/all_to_all | solution.py:406
  11.8 0.0 copy-done.5
  11.8 0.0 copy-start.3
  11.8 1.3 %copy.17 = f32[512,512]{0,1:T(8,128)} copy(f32[512,512]{1,0:T(8,128)S(1)} %copy-done.5) | data formatting | bytes 2097152 | tf_op args[0]
  13.2 0.0 copy-done.8
  13.2 0.2 reduce-window.8
  13.3 0.1 fusion.8
  13.4 0.0 copy-done.6
  13.5 0.1 fusion.7.mask_ref
  13.6 1.2 add_convert_fusion.1.counts_ref
  14.8 1.0 add_convert_fusion.spread_ref
  15.8 0.0 copy-done
  15.8 0.0 copy-done.1
  15.8 0.3 convolution_convert_fusion.dmixed_ref
  16.2 23.7 %all-to-all-done = bf16[32,32,512]{2,1,0:T(8,128)(2,1)S(1)} async-done(((bf16[32,32,512]{2,1,0:T(8,128)(2,1)}), bf16[32,32,512]{2,1,0:T(8,128)(2,1)S(1)}, u32[]{:S(2)}, u32[]{:S(2)}) %all-to-all-start) | async-done | bytes 1048608 | tf_op jit(solution)/shard_map/all_to_all | solution.py:406
  39.9 0.0 copy-done.3
  39.9 0.0 copy-start.2
  39.9 1.6 %copy-done.2 = bf16[512,2048]{1,0:T(8,128)(2,1)S(1)} copy-done((bf16[512,2048]{1,0:T(8,128)(2,1)S(1)}, bf16[512,2048]{1,0:T(8,128)(2,1)}, u32[]{:S(2)}) %copy-start.2) | copy-done | bytes 2097176
  41.5 5.1 %layer.1 = (bf16[256,512]{1,0:T(8,128)(2,1)}, bf16[2560,512]{1,0:T(8,128)(2,1)S(1)}, f32[1,512]{1,0:T(1,128)S(1)}, bf16[1024,512]{1,0:T(8,128)(2,1)S(1)}) custom-call(bf16[256,1024]{1,0:T(8,128)(2,1)S(1)} %add_convert_fusion.1.counts_ref, bf16[1024,256]{1,0:T(8,128)(2,1)S(1)} %add_convert_fusion.spread_ref, bf16[1024,512]{1,0:T(8,128)(2,1)S(1)} %bitcast.43, ...), custom_call_target="tpu_custom_call" | custom-call | flops 1744830464 | bytes 8388608 | tf_op jit(solution)/shard_map/layer/pallas_call | solution.py:154
  46.6 65.1 %exchange.1 = (bf16[32,32,512]{2,1,0:T(8,128)(2,1)S(1)}, f32[1,512]{1,0:T(1,128)S(1)}, bf16[32,80,512]{2,1,0:T(8,128)(2,1)S(1)}) custom-call(bf16[32,32,512]{2,1,0:T(8,128)(2,1)S(1)} %bitcast.42, f32[1,512]{1,0:T(1,128)S(1)} %get-tuple-element.15.gain_ref, bf16[32,80,512]{2,1,0:T(8,128)(2,1)S(1)} %bitcast.40), custom_call_target="tpu_custom_call" | custom-call | tf_op jit(solution)/shard_map/exchange/pallas_call | solution.py:358
  111.7 0.0 copy-start.7
  111.7 0.0 copy-start.4
  111.7 1.0 multiply_reduce_fusion
  112.7 0.6 broadcast_multiply_fusion
  113.3 0.0 copy-done.7
  113.3 0.6 sqrt_add_fusion
  113.9 0.0 copy-done.4
  113.9 1.2 %divide_subtract_fusion = f32[512,512]{0,1:T(8,128)} fusion(f32[512,512]{0,1:T(8,128)S(1)} %copy-done.4, f32[512,512]{0,1:T(8,128)S(1)} %get-tuple-element.56, f32[512]{0:T(512)S(1)} %get-tuple-element.32), kind=kLoop, calls=%fused_computation.11 | loop fusion | flops 786432 | bytes 3147776 | tf_op jit(solution)/shard_map/sub | solution.py:438
  115.1 2.5 %copy.18 = f32[512,512]{1,0:T(8,128)} copy(f32[512,512]{0,1:T(8,128)} %divide_subtract_fusion) | data formatting | bytes 2097152
  117.6 1.7 %multiply_bitcast_fusion = (f32[512,512]{1,0:T(8,128)}, f32[512,512]{1,0:T(8,128)S(1)}, f32[512,512]{1,0:T(8,128)S(1)}, f32[512,512]{1,0:T(8,128)S(1)}, f32[512,512]{1,0:T(8,128)S(1)}) fusion(bf16[5,512,512]{2,1,0:T(8,128)(2,1)S(1)} %bitcast.41), kind=kLoop, calls=%fused_computation.6 | loop fusion | flops 2621440 | bytes 7864320 | tf_op jit(solution)/shard_map/mul | solution.py:445
  119.4 2.4 %pad_maximum_fusion = f32[512,2048]{1,0:T(8,128)} fusion(f32[512,512]{1,0:T(8,128)S(1)} %get-tuple-element.35, f32[512,512]{1,0:T(8,128)S(1)} %get-tuple-element.36, f32[512,512]{1,0:T(8,128)S(1)} %get-tuple-element.37, f32[512,512]{1,0:T(8,128)S(1)} %get-tuple-element.38), kind=kLoop, calls=%fused_computation | loop fusion | flops 3145728 | bytes 8388608 | tf_op jit(solution)/shard_map/concatenate | solution.py:444
  (2 shorter events, 0.0 us)
Async XLA Ops:
  0.6 11.2 %copy-start.5 = (f32[512,512]{1,0:T(8,128)S(1)}, f32[512,512]{1,0:T(8,128)}, u32[]{:S(2)}) copy-start(f32[512,512]{1,0:T(8,128)} %param.9) | copy-start | bytes 3145732
  4.5 8.7 %copy-start.8 = (s32[1,2]{1,0:T(1,128)S(1)}, s32[1,2]{1,0:T(1,128)}, u32[]{:S(2)}) copy-start(s32[1,2]{1,0:T(1,128)} %param.13) | copy-start | bytes 28
  4.5 8.9 %copy-start.6 = (s32[256,8]{0,1:T(8,128)S(1)}, s32[256,8]{0,1:T(8,128)}, u32[]{:S(2)}) copy-start(s32[256,8]{0,1:T(8,128)} %param.12) | copy-start | bytes 24580
  4.5 11.3 %copy-start = (bf16[512,512]{1,0:T(8,128)(2,1)S(1)}, bf16[512,512]{1,0:T(8,128)(2,1)}, u32[]{:S(2)}) copy-start(bf16[512,512]{1,0:T(8,128)(2,1)} %wout_ref.1) | copy-start | bytes 1572868
  4.5 11.3 %copy-start.1 = (bf16[256,512]{1,0:T(8,128)(2,1)S(1)}, bf16[256,512]{1,0:T(8,128)(2,1)}, u32[]{:S(2)}) copy-start(bf16[256,512]{1,0:T(8,128)(2,1)} %cot_ref.1) | copy-start | bytes 786436
  4.5 35.4 %all-to-all-start = ((bf16[32,32,512]{2,1,0:T(8,128)(2,1)}), bf16[32,32,512]{2,1,0:T(8,128)(2,1)S(1)}, u32[]{:S(2)}, u32[]{:S(2)}) async-start(bf16[32,32,512]{2,1,0:T(8,128)(2,1)} %bitcast.46), calls=%async_computation | async-start | bytes 2097152 | tf_op jit(solution)/shard_map/all_to_all | solution.py:406
  11.8 28.0 %copy-start.3 = (f32[512]{0:T(512)S(1)}, f32[512]{0:T(512)}, u32[]{:S(2)}) copy-start(f32[512]{0:T(512)} %param.16) | copy-start | bytes 6148
  39.9 1.6 %copy-start.2 = (bf16[512,2048]{1,0:T(8,128)(2,1)S(1)}, bf16[512,2048]{1,0:T(8,128)(2,1)}, u32[]{:S(2)}) copy-start(bf16[512,2048]{1,0:T(8,128)(2,1)} %win_ref.1) | copy-start | bytes 6291460
  111.7 1.6 %copy-start.7 = (f32[512]{0:T(512)S(1)}, f32[512]{0:T(512)}, u32[]{:S(2)}) copy-start(f32[512]{0:T(512)} %param.10) | copy-start | bytes 6148
  111.7 2.2 %copy-start.4 = (f32[512,512]{0,1:T(8,128)S(1)}, f32[512,512]{0,1:T(8,128)}, u32[]{:S(2)}) copy-start(f32[512,512]{0,1:T(8,128)} %copy.17) | copy-start | bytes 3145732
